TPU v7x, 8 devices: a whole 2x2x1 slice. The times are simulated.
8 devices in a mesh: dp: 1 (over z), pool: 2 (over y), ep: 4 (over x, core).
Axes of the slice: x: 2, y: 2, z: 1, core: 2. Of those that a mesh axis runs over, the one named last changes fastest.
Arguments:
- hidden: bfloat16 [128, 1024], P(('dp', 'ep'))
- k_cache: bfloat16 [2, 128, 128, 2, 128], P(None, ('dp', 'ep'))
- v_cache: bfloat16 [2, 128, 128, 2, 128], P(None, ('dp', 'ep'))
- lengths: int32 [128], P(('dp', 'ep'))
- expert_ids: int32 [2, 128, 8], P(None, ('dp', 'ep'))
- w_query: bfloat16 [2, 1024, 2048], replicated
- w_key: bfloat16 [2, 1024, 256], replicated
- w_value: bfloat16 [2, 1024, 256], replicated
- w_out: bfloat16 [2, 2048, 1024], replicated
- w_router: float32 [2, 1024, 64], replicated
- w_gate: bfloat16 [2, 64, 1024, 768], P(None, 'ep')
- w_up: bfloat16 [2, 64, 1024, 768], P(None, 'ep')
- w_down: bfloat16 [2, 64, 768, 1024], P(None, 'ep')
Outputs:
- output: bfloat16 [128, 1024], P(('dp', 'ep'))
All inputs are finite; a program needn't handle non-finite values.
Results may differ from a plain program's by a relative error of at most 0.0178775.
Values are sent between devices in bfloat16 or wider.
A program may use at most 1 GiB of HBM per device.

v0:
```python
import functools
import math

import jax
import jax.numpy as jnp
from jax import lax
from jax.experimental import pallas as pl
from jax.experimental.pallas import tpu as pltpu
from jax.sharding import PartitionSpec as P

EPSILON = 1e-6
ROPE_BASE = 10000.0
MESH = pl.DeviceIdType.MESH
F32 = jnp.float32
BF16 = jnp.bfloat16
NT = (((1,), (1,)), ((), ()))


def rms_normed(values):
    return values * lax.rsqrt(jnp.mean(values * values, axis=-1, keepdims=True) + EPSILON)


def kernel(cfg, hid, kc, vc, lens, ids, wq, wk, wv, wo, wr, wg, wu, wd, out,
           wq_s, wk_s, wv_s, wo_s, wr_s, kb, vb, w1_s, w3_s, w2_s,
           x_s, a_s, ids_s, idt_s, q_s, s_s, o_s,
           u_all, g_all, gb_s, inner_s, part, rbuf, xfin,
           sem_a, sem_w, sem_w2, sem_u, sem_us, sem_g, sem_gs, sem_c, sem_cs, sem_x, sem_out):
    layers, n_pool, n_ep, tok, heads, kvh, hd, seq, n_loc, ff, model = cfg
    n_dev = n_pool * n_ep
    n_chunk, _, _, cw = w2_s.shape
    p = lax.axis_index("pool")
    ep = lax.axis_index("ep")
    me = p * n_ep + ep
    row0 = pl.multiple_of(p * tok, tok)

    def peer(j):
        d = lax.rem(me + j, n_dev)
        return d, {"pool": d // n_ep, "ep": lax.rem(d, n_ep)}

    barrier = pltpu.get_barrier_semaphore()
    for j in range(1, n_dev):
        pl.semaphore_signal(barrier, inc=1, device_id=peer(j)[1], device_id_type=MESH)

    def attn_copy(l, k):
        src, dst = [
            (lambda: wq.at[l], wq_s), (lambda: wk.at[l], wk_s), (lambda: wv.at[l], wv_s),
            (lambda: kc.at[l, pl.ds(row0, tok)], kb), (lambda: vc.at[l, pl.ds(row0, tok)], vb),
            (lambda: wo.at[l], wo_s), (lambda: wr.at[l], wr_s),
        ][k]
        return pltpu.make_async_copy(src(), dst, sem_a.at[k])

    def up_copies(l, i):
        e = p * n_loc + i
        return [
            pltpu.make_async_copy(wg.at[l, e], w1_s.at[i], sem_w.at[0, i]),
            pltpu.make_async_copy(wu.at[l, e], w3_s.at[i], sem_w.at[1, i]),
        ]

    def down_copy(l, n):
        return pltpu.make_async_copy(
            wd.at[l, pl.ds(p * n_loc, n_loc), :, pl.ds(n * cw, cw)], w2_s.at[n], sem_w2.at[n])

    hid_copy = pltpu.make_async_copy(hid.at[pl.ds(row0, tok)], xfin.at[0], sem_a.at[7])
    ids_copy = pltpu.make_async_copy(ids, ids_s, sem_a.at[8])
    hid_copy.start()
    ids_copy.start()
    for k in range(7):
        attn_copy(0, k).start()
    for i in range(n_loc):
        for c in up_copies(0, i):
            c.start()
    for n in range(n_chunk):
        down_copy(0, n).start()

    rows = lax.broadcasted_iota(jnp.int32, (tok, hd), 0)
    lanes = lax.broadcasted_iota(jnp.int32, (tok, hd), 1)
    len_i = jnp.zeros((tok, hd), jnp.int32)
    for t in range(tok):
        len_i = jnp.where(rows == t, lens[p * tok + t], len_i)
    half = hd // 2
    pair = jnp.where(lanes < half, lanes, lanes - half).astype(F32)
    freq = jnp.exp(pair * (-2.0 * math.log(ROPE_BASE) / hd))
    angle = len_i.astype(F32) * freq
    cosine = jnp.cos(angle)
    sine = jnp.sin(angle)
    sine = jnp.where(lanes < half, -sine, sine)

    def rotary(v):
        return v * cosine + pltpu.roll(v, half, 1) * sine

    ids_copy.wait()
    for l in range(layers):
        idf = jnp.concatenate([ids_s[l].astype(F32), jnp.zeros((ids_s.shape[1], 128 - ids_s.shape[2]), F32)], axis=1)
        idt_s[l] = jnp.transpose(idf)
    hid_copy.wait()
    x_s[...] = xfin[0].astype(F32)

    scale = hd ** -0.5
    group = heads // kvh

    def attention(l):
        x = x_s[...]
        h = rms_normed(x).astype(BF16)
        attn_copy(l, 0).wait()
        qc = 256
        for c in range(heads * hd // qc):
            qq = jnp.dot(h, wq_s[:, c * qc:(c + 1) * qc], preferred_element_type=F32)
            for s in range(qc // hd):
                hh = c * (qc // hd) + s
                q_s[hh * tok:(hh + 1) * tok, :] = rotary(qq[:, s * hd:(s + 1) * hd]).astype(BF16).astype(F32)
        attn_copy(l, 1).wait()
        kk = jnp.dot(h, wk_s[...], preferred_element_type=F32)
        k_new = [rotary(kk[:, s * hd:(s + 1) * hd]).astype(BF16).astype(F32) for s in range(kvh)]
        attn_copy(l, 2).wait()
        vv = jnp.dot(h, wv_s[...], preferred_element_type=F32).astype(BF16).astype(F32)
        v_new = [vv[:, s * hd:(s + 1) * hd] for s in range(kvh)]
        attn_copy(l, 3).wait()
        for t in range(tok):
            qt = q_s[pl.ds(t, heads, stride=tok), :].astype(BF16)
            st = lax.dot_general(qt, kb[t], NT, preferred_element_type=F32) * scale
            for b in range(kvh * seq // 128):
                s_s[b, pl.ds(t, heads, stride=tok), :] = st[:, b * 128:(b + 1) * 128]
        lane = lax.broadcasted_iota(jnp.int32, (tok, 128), 1)
        w_new = []
        den = []
        for hh in range(heads):
            kv = hh // group
            sl = slice(hh * tok, (hh + 1) * tok)
            sn = jnp.sum(q_s[sl, :] * k_new[kv], axis=-1, keepdims=True) * scale
            blocks = []
            for b in range(kvh * seq // 128):
                col = lane + b * 128
                ok = (lax.rem(col, kvh) == kv) & (col // kvh < len_i)
                blocks.append(jnp.where(ok, s_s[b, sl, :], -jnp.inf))
            top = functools.reduce(jnp.maximum, blocks)
            peak = jnp.maximum(jnp.max(top, axis=-1, keepdims=True), sn)
            ws = [jnp.exp(v - peak) for v in blocks]
            for b, w in enumerate(ws):
                s_s[b, sl, :] = w
            wn = jnp.exp(sn - peak)
            w_new.append(wn)
            den.append(jnp.sum(functools.reduce(jnp.add, ws), axis=-1, keepdims=True) + wn)
        attn_copy(l, 4).wait()
        for t in range(tok):
            pt = jnp.concatenate(
                [s_s[b, pl.ds(t, heads, stride=tok), :] for b in range(kvh * seq // 128)], axis=1).astype(BF16)
            o_s[pl.ds(t, heads, stride=tok), :] = jnp.dot(pt, vb[t], preferred_element_type=F32)
        pieces = []
        for hh in range(heads):
            sl = slice(hh * tok, (hh + 1) * tok)
            mixed = o_s[sl, :] + w_new[hh].astype(BF16).astype(F32) * v_new[hh // group]
            pieces.append((mixed / den[hh]).astype(BF16))
        o = jnp.concatenate(pieces, axis=1)
        attn_copy(l, 5).wait()
        oc = 256
        for c in range(model // oc):
            sl = slice(c * oc, (c + 1) * oc)
            a_s[:, sl] = (x[:, sl] + jnp.dot(o, wo_s[:, sl], preferred_element_type=F32)).astype(BF16).astype(F32)

    def u_copy(l, j, src):
        d, dev = peer(j)
        return pltpu.make_async_remote_copy(
            src_ref=u_all.at[l, src], dst_ref=u_all.at[l, src], send_sem=sem_us.at[l, j], recv_sem=sem_u.at[l, src],
            device_id=dev, device_id_type=MESH)

    def g_copy(l, j, src):
        d, dev = peer(j)
        return pltpu.make_async_remote_copy(
            src_ref=g_all.at[l, src], dst_ref=g_all.at[l, src], send_sem=sem_gs.at[l, j], recv_sem=sem_g.at[l, src],
            device_id=dev, device_id_type=MESH)

    def c_copy(l, n, j, src):
        d, dev = peer(j)
        return pltpu.make_async_remote_copy(
            src_ref=part.at[l, n, d], dst_ref=rbuf.at[l, n, src], send_sem=sem_cs.at[l, n, j], recv_sem=sem_c.at[l, n, src],
            device_id=dev, device_id_type=MESH)

    def route(l):
        u = rms_normed(a_s[...]).astype(BF16)
        u_all[l, me] = u
        for j in range(1, n_dev):
            u_copy(l, j, me).start()
        attn_copy(l, 6).wait()
        rest = wr_s[...]
        n_exp = rest.shape[0]
        logits = jnp.zeros((tok, n_exp), F32)
        for _ in range(3):
            piece = rest.astype(BF16)
            rest = rest - piece.astype(F32)
            logits = logits + lax.dot_general(u, piece, NT, preferred_element_type=F32)
        mine = idt_s[l, pl.ds(row0, tok), :]
        expert = lax.broadcasted_iota(jnp.int32, (tok, n_exp), 1).astype(F32)
        chosen = jnp.zeros((tok, n_exp), jnp.bool_)
        for k in range(mine.shape[1]):
            chosen = chosen | (mine[:, k:k + 1] == expert)
        masked = jnp.where(chosen, logits, -jnp.inf)
        w = jnp.exp(masked - jnp.max(masked, axis=-1, keepdims=True))
        gates = w / jnp.sum(w, axis=-1, keepdims=True)
        g_all[l, me] = jnp.concatenate([gates, jnp.zeros((tok, 128 - n_exp), F32)], axis=1)
        for j in range(1, n_dev):
            g_copy(l, j, me).start()

    def experts(l):
        for j in range(1, n_dev):
            u_copy(l, j, peer(j)[0]).wait_recv()
        n_tok = n_dev * tok

        def up_step(i, carry):
            for c in up_copies(l, i):
                c.wait()
            ub = u_all[l].reshape(n_tok, model)
            fc = 256
            for n in range(ff // fc):
                sl = slice(n * fc, (n + 1) * fc)
                one = jnp.dot(ub, w1_s[i, :, sl], preferred_element_type=F32)
                three = jnp.dot(ub, w3_s[i, :, sl], preferred_element_type=F32)
                inner_s[i, :, sl] = (jax.nn.silu(one) * three).astype(BF16)
            if l + 1 < layers:
                for c in up_copies(l + 1, i):
                    c.start()
            return carry

        lax.fori_loop(0, n_loc, up_step, 0)
        for j in range(1, n_dev):
            g_copy(l, j, peer(j)[0]).wait_recv()
        gates = g_all[l].reshape(n_tok, 128)
        lane = lax.broadcasted_iota(jnp.int32, (n_tok, 128), 1)
        first = (ep * n_pool + p) * n_loc
        for i in range(n_loc):
            g = jnp.sum(jnp.where(lane == first + i, gates, 0.0), axis=-1, keepdims=True)
            gb_s[i] = jnp.broadcast_to(g, (n_tok, 128))

        def down_step(n, carry):
            down_copy(l, n).wait()
            acc = [jnp.zeros((n_tok, 128), F32) for _ in range(cw // 128)]
            for i in range(n_loc):
                y = jnp.dot(inner_s[i], w2_s[n, i], preferred_element_type=F32).astype(BF16).astype(F32)
                g = gb_s[i]
                for b in range(cw // 128):
                    acc[b] = acc[b] + jnp.where(g > 0.0, g * y[:, b * 128:(b + 1) * 128], 0.0)
            for b in range(cw // 128):
                part[l, n, :, :, b * 128:(b + 1) * 128] = acc[b].reshape(n_dev, tok, 128)
            for j in range(1, n_dev):
                c_copy(l, n, j, me).start()
            if l + 1 < layers:
                down_copy(l + 1, n).start()
            return carry

        lax.fori_loop(0, n_chunk, down_step, 0)

    other = 1 - p

    def x_copy(n):
        return pltpu.make_async_remote_copy(
            src_ref=xfin.at[p, :, pl.ds(n * cw, cw)], dst_ref=xfin.at[p, :, pl.ds(n * cw, cw)],
            send_sem=sem_x.at[0, n], recv_sem=sem_x.at[1, n],
            device_id={"pool": other, "ep": ep}, device_id_type=MESH)

    def x_arrival(n):
        return pltpu.make_async_remote_copy(
            src_ref=xfin.at[other, :, pl.ds(n * cw, cw)], dst_ref=xfin.at[other, :, pl.ds(n * cw, cw)],
            send_sem=sem_x.at[0, n], recv_sem=sem_x.at[1, n],
            device_id={"pool": other, "ep": ep}, device_id_type=MESH)

    def combine(l):
        for n in range(n_chunk):
            total = part[l, n, me]
            for j in range(1, n_dev):
                src = peer(j)[0]
                c_copy(l, n, j, src).wait_recv()
                total = total + rbuf[l, n, src]
            sl = slice(n * cw, (n + 1) * cw)
            x = (a_s[:, sl] + total).astype(BF16)
            if l + 1 < layers:
                x_s[:, sl] = x.astype(F32)
            else:
                xfin[p, :, sl] = x
                x_copy(n).start()

    for l in range(layers):
        attention(l)
        if l == 0:
            pl.semaphore_wait(barrier, n_dev - 1)
        route(l)
        if l + 1 < layers:
            for k in range(7):
                attn_copy(l + 1, k).start()
        experts(l)
        combine(l)

    own = pltpu.make_async_copy(xfin.at[p], out.at[pl.ds(row0, tok)], sem_out.at[0])
    own.start()
    for n in range(n_chunk):
        x_arrival(n).wait_recv()
    partner = pltpu.make_async_copy(xfin.at[other], out.at[pl.ds(pl.multiple_of(other * tok, tok), tok)], sem_out.at[1])
    partner.start()
    for n in range(n_chunk):
        x_copy(n).wait_send()
    for l in range(layers):
        for j in range(1, n_dev):
            u_copy(l, j, me).wait_send()
            g_copy(l, j, me).wait_send()
            for n in range(n_chunk):
                c_copy(l, n, j, me).wait_send()
    own.wait()
    partner.wait()


def solution(mesh):
    n_pool = mesh.shape["pool"]
    n_ep = mesh.shape["ep"]
    n_dev = n_pool * n_ep

    def body(hidden, k_cache, v_cache, lengths, expert_ids, w_query, w_key, w_value, w_out, w_router, w_gate, w_up, w_down):
        layers, n_tok, seq, kvh, hd = k_cache.shape
        tok = n_tok // n_pool
        model = hidden.shape[1]
        heads = w_query.shape[2] // hd
        n_loc = w_gate.shape[1] // n_pool
        ff = w_gate.shape[3]
        n_exp = w_router.shape[2]
        topk = expert_ids.shape[2]
        cw = 256
        n_chunk = model // cw
        kflat = k_cache.reshape(layers, n_tok, seq * kvh, hd)
        vflat = v_cache.reshape(layers, n_tok, seq * kvh, hd)
        ids = jnp.swapaxes(expert_ids, 1, 2)
        router = jnp.swapaxes(w_router, 1, 2)
        cfg = (layers, n_pool, n_ep, tok, heads, kvh, hd, seq, n_loc, ff, model)
        any_spec = pl.BlockSpec(memory_space=pl.ANY)
        smem_spec = pl.BlockSpec(memory_space=pltpu.SMEM)
        vm = pltpu.VMEM
        dma = pltpu.SemaphoreType.DMA
        return pl.pallas_call(
            functools.partial(kernel, cfg),
            out_shape=jax.ShapeDtypeStruct((n_tok, model), BF16),
            in_specs=[any_spec] * 3 + [smem_spec] + [any_spec] * 9,
            out_specs=any_spec,
            scratch_shapes=[
                vm((model, heads * hd), BF16), vm((model, kvh * hd), BF16), vm((model, kvh * hd), BF16),
                vm((heads * hd, model), BF16), vm((n_exp, model), F32),
                vm((tok, seq * kvh, hd), BF16), vm((tok, seq * kvh, hd), BF16),
                vm((n_loc, model, ff), BF16), vm((n_loc, model, ff), BF16), vm((n_chunk, n_loc, ff, cw), BF16),
                vm((tok, model), F32), vm((tok, model), F32), vm((layers, topk, n_tok), jnp.int32), vm((layers, 128, topk), F32),
                vm((heads * tok, hd), F32), vm((kvh * seq // 128, heads * tok, 128), F32), vm((heads * tok, hd), F32),
                vm((layers, n_dev, tok, model), BF16), vm((layers, n_dev, tok, 128), F32), vm((n_loc, n_dev * tok, 128), F32),
                vm((n_loc, n_dev * tok, ff), BF16), vm((layers, n_chunk, n_dev, tok, cw), F32),
                vm((layers, n_chunk, n_dev, tok, cw), F32), vm((n_pool, tok, model), BF16),
                dma((9,)), dma((2, n_loc)), dma((n_chunk,)), dma((layers, n_dev)), dma((layers, n_dev)),
                dma((layers, n_dev)), dma((layers, n_dev)), dma((layers, n_chunk, n_dev)), dma((layers, n_chunk, n_dev)),
                dma((2, n_chunk)), dma((2,)),
            ],
            compiler_params=pltpu.CompilerParams(
                collective_id=0, has_side_effects=True, vmem_limit_bytes=66 * 1024 * 1024 - 2 * 1024 * 1024 - 65536),
        )(hidden, kflat, vflat, lengths, ids, w_query, w_key, w_value, w_out, router, w_gate, w_up, w_down)

    rows_spec = ("dp", "ep")
    in_specs = (P(rows_spec, None), P(None, rows_spec), P(None, rows_spec), P(rows_spec), P(None, rows_spec, None), P(), P(), P(), P(), P(), P(None, "ep"), P(None, "ep"), P(None, "ep"))
    return jax.shard_map(body, mesh=mesh, in_specs=in_specs, out_specs=P(rows_spec, None), check_vma=False)
```

profile of v0, /device:TPU:0, one launch (start us, length us, event | category | flops | bytes accessed | tf_op | source)
XLA Modules:
  0.0 63.3 jit_solution(3305596306536573385)
XLA Ops:
  0.0 61.8 %shard_map.127 = bf16[32,1024]{1,0:T(8,128)(2,1)} custom-call(bf16[32,1024]{1,0:T(8,128)(2,1)} %hid.1, bf16[2,32,256,128]{3,2,1,0:T(8,128)(2,1)} %bitcast.4, bf16[2,32,256,128]{3,2,1,0:T(8,128)(2,1)} %bitcast.5, s32[32]{0:T(128)} %lens.1, s32[2,8,32]{2,1,0:T(8,128)} %bitcast.7, bf16[2,1024,2048]{2,1,0:T(8,128)(2,1)} %wq.1, bf16[2,1024,256]{2,1,0:T(8,128)(2,1)} %wk.1, ...), custom_call_target="tpu_custom_call" | custom-call | tf_op jit(solution)/shard_map/pallas_call | solution.py:334
  61.8 1.5 %copy.15 = bf16[32,1024]{1,0:T(8,128)(2,1)} copy(bf16[32,1024]{1,0:T(8,128)(2,1)} %shard_map.127) | data formatting | bytes 131072
where the time goes:
time: 63.4 us; the launch traced here: 63.3 us
  Pallas kernels  61.8 us (97%)
  local copies, waits for them, and re-layouts  1.47 us (2%)
    pallas_call x1, Pallas kernels, body(): pl.pallas_call(functools.partial(kernel, cfg), out_shape=jax.ShapeDtypeSt...  61.8 us
    unnamed x1, local copies, waits for them, and re-layouts  1.47 us

commit v1 on v0

v1 whole, which is shorter than its diff:
```python
import functools
import math

import jax
import jax.numpy as jnp
from jax import lax
from jax.experimental import pallas as pl
from jax.experimental.pallas import tpu as pltpu
from jax.sharding import PartitionSpec as P

EPSILON = 1e-6
ROPE_BASE = 10000.0
MESH = pl.DeviceIdType.MESH
F32 = jnp.float32
BF16 = jnp.bfloat16
NT = (((1,), (1,)), ((), ()))


def rms_normed(values):
    return values * lax.rsqrt(jnp.mean(values * values, axis=-1, keepdims=True) + EPSILON)


def kernel(cfg, hid, kc, vc, lens, ids, wq, wk, wv, wo, wr, wg, wu, wd, xfin,
           wq_s, wk_s, wv_s, wo_s, wr_s, kb, vb, w1_s, w3_s, w2_s,
           x_s, a_s, ids_s, idt_s, q_s, s_s, o_s,
           u_all, g_all, gb_s, inner_s, part, sbuf, red, rbuf, hid_s,
           sem_a, sem_w, sem_w2, sem_u, sem_us, sem_g, sem_gs, sem_d, sem_ds, sem_c, sem_cs, sem_x):
    layers, n_pool, n_ep, tok, heads, kvh, hd, seq, n_loc, ff, model = cfg
    n_dev = n_pool * n_ep
    n_chunk, _, _, cw = w2_s.shape
    p = lax.axis_index("pool")
    ep = lax.axis_index("ep")
    me = p * n_ep + ep
    row0 = pl.multiple_of(p * tok, tok)

    cx = ep // 2
    cc = lax.rem(ep, 2)

    def peer(dy, dx, dc):
        y, e = lax.rem(p + dy, 2), lax.rem(cx + dx, 2) * 2 + lax.rem(cc + dc, 2)
        return y * n_ep + e, {"pool": y, "ep": e}

    others = [(1, 1, 1), (1, 1, 0), (0, 1, 1), (1, 0, 1), (0, 1, 0), (1, 0, 0), (0, 0, 1)]
    chips = [(0, 0), (0, 1), (1, 0), (1, 1)]

    barrier = pltpu.get_barrier_semaphore()
    for rel in others:
        pl.semaphore_signal(barrier, inc=1, device_id=peer(*rel)[1], device_id_type=MESH)

    def attn_copy(l, k):
        src, dst = [
            (lambda: wq.at[l], wq_s), (lambda: wk.at[l], wk_s), (lambda: wv.at[l], wv_s),
            (lambda: kc.at[l, pl.ds(row0, tok)], kb), (lambda: vc.at[l, pl.ds(row0, tok)], vb),
            (lambda: wo.at[l], wo_s), (lambda: wr.at[l], wr_s),
        ][k]
        return pltpu.make_async_copy(src(), dst, sem_a.at[k])

    def up_copies(l, i):
        e = p * n_loc + i
        return [
            pltpu.make_async_copy(wg.at[l, e], w1_s.at[i], sem_w.at[0, i]),
            pltpu.make_async_copy(wu.at[l, e], w3_s.at[i], sem_w.at[1, i]),
        ]

    def down_copy(l, n):
        return pltpu.make_async_copy(
            wd.at[l, pl.ds(p * n_loc, n_loc), :, pl.ds(n * cw, cw)], w2_s.at[n], sem_w2.at[n])

    hid_copy = pltpu.make_async_copy(hid.at[pl.ds(row0, tok)], hid_s, sem_a.at[7])
    ids_copy = pltpu.make_async_copy(ids, ids_s, sem_a.at[8])
    hid_copy.start()
    ids_copy.start()
    for k in range(7):
        attn_copy(0, k).start()

    def start_up(l, lo, hi):
        for i in range(lo, hi):
            for c in up_copies(l, i):
                c.start()

    rows = lax.broadcasted_iota(jnp.int32, (tok, hd), 0)
    lanes = lax.broadcasted_iota(jnp.int32, (tok, hd), 1)
    len_i = jnp.zeros((tok, hd), jnp.int32)
    for t in range(tok):
        len_i = jnp.where(rows == t, lens[p * tok + t], len_i)
    half = hd // 2
    pair = jnp.where(lanes < half, lanes, lanes - half).astype(F32)
    freq = jnp.exp(pair * (-2.0 * math.log(ROPE_BASE) / hd))
    angle = len_i.astype(F32) * freq
    cosine = jnp.cos(angle)
    sine = jnp.sin(angle)
    sine = jnp.where(lanes < half, -sine, sine)

    def rotary(v):
        return v * cosine + pltpu.roll(v, half, 1) * sine

    with jax.named_scope("idswait"):
        ids_copy.wait()
    for l in range(layers):
        idf = jnp.concatenate([ids_s[l].astype(F32), jnp.zeros((ids_s.shape[1], 128 - ids_s.shape[2]), F32)], axis=1)
        idt_s[l] = jnp.transpose(idf)
    with jax.named_scope("hidwait"):
        hid_copy.wait()
    x_s[...] = hid_s[...].astype(F32)

    scale = hd ** -0.5
    group = heads // kvh

    def attention(l):
        x = x_s[...]
        h = rms_normed(x).astype(BF16)
        with jax.named_scope(f"await0_{l}"):
            for k in range(3 if l == 0 else 7):
                attn_copy(l, k).wait()
        if l == 0:
            start_up(0, 0, 2)
        qc = 256
        for c in range(heads * hd // qc):
            qq = jnp.dot(h, wq_s[:, c * qc:(c + 1) * qc], preferred_element_type=F32)
            for s in range(qc // hd):
                hh = c * (qc // hd) + s
                q_s[hh * tok:(hh + 1) * tok, :] = rotary(qq[:, s * hd:(s + 1) * hd]).astype(BF16).astype(F32)
        kk = jnp.dot(h, wk_s[...], preferred_element_type=F32)
        k_new = [rotary(kk[:, s * hd:(s + 1) * hd]).astype(BF16).astype(F32) for s in range(kvh)]
        vv = jnp.dot(h, wv_s[...], preferred_element_type=F32).astype(BF16).astype(F32)
        v_new = [vv[:, s * hd:(s + 1) * hd] for s in range(kvh)]
        if l == 0:
            with jax.named_scope(f"await3_{l}"):
                attn_copy(l, 3).wait()
                attn_copy(l, 4).wait()
            start_up(0, 2, 4)
        for t in range(tok):
            qt = q_s[pl.ds(t, heads, stride=tok), :].astype(BF16)
            st = lax.dot_general(qt, kb[t], NT, preferred_element_type=F32) * scale
            for b in range(kvh * seq // 128):
                s_s[b, pl.ds(t, heads, stride=tok), :] = st[:, b * 128:(b + 1) * 128]
        lane = lax.broadcasted_iota(jnp.int32, (tok, 128), 1)
        w_new = []
        den = []
        for hh in range(heads):
            kv = hh // group
            sl = slice(hh * tok, (hh + 1) * tok)
            sn = jnp.sum(q_s[sl, :] * k_new[kv], axis=-1, keepdims=True) * scale
            blocks = []
            for b in range(kvh * seq // 128):
                col = lane + b * 128
                ok = (lax.rem(col, kvh) == kv) & (col // kvh < len_i)
                blocks.append(jnp.where(ok, s_s[b, sl, :], -jnp.inf))
            top = functools.reduce(jnp.maximum, blocks)
            peak = jnp.maximum(jnp.max(top, axis=-1, keepdims=True), sn)
            ws = [jnp.exp(v - peak) for v in blocks]
            for b, w in enumerate(ws):
                s_s[b, sl, :] = w
            wn = jnp.exp(sn - peak)
            w_new.append(wn)
            den.append(jnp.sum(functools.reduce(jnp.add, ws), axis=-1, keepdims=True) + wn)
        for t in range(tok):
            pt = jnp.concatenate(
                [s_s[b, pl.ds(t, heads, stride=tok), :] for b in range(kvh * seq // 128)], axis=1).astype(BF16)
            o_s[pl.ds(t, heads, stride=tok), :] = jnp.dot(pt, vb[t], preferred_element_type=F32)
        pieces = []
        for hh in range(heads):
            sl = slice(hh * tok, (hh + 1) * tok)
            mixed = o_s[sl, :] + w_new[hh].astype(BF16).astype(F32) * v_new[hh // group]
            pieces.append((mixed / den[hh]).astype(BF16))
        o = jnp.concatenate(pieces, axis=1)
        if l == 0:
            with jax.named_scope(f"await5_{l}"):
                attn_copy(l, 5).wait()
            start_up(0, 4, n_loc)
            for n in range(n_chunk):
                down_copy(0, n).start()
        oc = 256
        for c in range(model // oc):
            sl = slice(c * oc, (c + 1) * oc)
            a_s[:, sl] = (x[:, sl] + jnp.dot(o, wo_s[:, sl], preferred_element_type=F32)).astype(BF16).astype(F32)

    def u_copy(l, j, src):
        return pltpu.make_async_remote_copy(
            src_ref=u_all.at[l, src], dst_ref=u_all.at[l, src], send_sem=sem_us.at[l, j], recv_sem=sem_u.at[l, j],
            device_id=peer(*others[j])[1], device_id_type=MESH)

    def g_copy(l, j, src):
        return pltpu.make_async_remote_copy(
            src_ref=g_all.at[l, src], dst_ref=g_all.at[l, src], send_sem=sem_gs.at[l, j], recv_sem=sem_g.at[l, j],
            device_id=peer(*others[j])[1], device_id_type=MESH)

    def d_copy(l, n, k):
        dest = peer(0, 0, 1)[0] if k == 0 else peer(*chips[k], 0)[0]
        return pltpu.make_async_remote_copy(
            src_ref=part.at[l, n, dest], dst_ref=sbuf.at[l, n, k], send_sem=sem_ds.at[l, n, k], recv_sem=sem_d.at[l, n, k],
            device_id=peer(0, 0, 1)[1], device_id_type=MESH)

    def c_copy(l, n, k):
        return pltpu.make_async_remote_copy(
            src_ref=red.at[l, n, k], dst_ref=rbuf.at[l, n, k], send_sem=sem_cs.at[l, n, k], recv_sem=sem_c.at[l, n, k],
            device_id=peer(*chips[k], 1)[1], device_id_type=MESH)

    far_first = (3, 1, 2)

    def route(l):
        u = rms_normed(a_s[...]).astype(BF16)
        u_all[l, me] = u
        for j in range(len(others)):
            u_copy(l, j, me).start()
        if l == 0:
            with jax.named_scope(f"await6_{l}"):
                attn_copy(l, 6).wait()
        rest = wr_s[...]
        n_exp = rest.shape[0]
        logits = jnp.zeros((tok, n_exp), F32)
        for _ in range(3):
            piece = rest.astype(BF16)
            rest = rest - piece.astype(F32)
            logits = logits + lax.dot_general(u, piece, NT, preferred_element_type=F32)
        mine = idt_s[l, pl.ds(row0, tok), :]
        expert = lax.broadcasted_iota(jnp.int32, (tok, n_exp), 1).astype(F32)
        chosen = jnp.zeros((tok, n_exp), jnp.bool_)
        for k in range(mine.shape[1]):
            chosen = chosen | (mine[:, k:k + 1] == expert)
        masked = jnp.where(chosen, logits, -jnp.inf)
        w = jnp.exp(masked - jnp.max(masked, axis=-1, keepdims=True))
        gates = w / jnp.sum(w, axis=-1, keepdims=True)
        g_all[l, me] = jnp.concatenate([gates, jnp.zeros((tok, 128 - n_exp), F32)], axis=1)
        for j in range(len(others)):
            g_copy(l, j, me).start()

    n_tok = n_dev * tok
    fc = 256
    per = 4

    def up_block(l, g):
        with jax.named_scope(f"upwait{l}"):
            for i in range(g * per, (g + 1) * per):
                for c in up_copies(l, i):
                    c.wait()
        for i in range(g * per, (g + 1) * per):
            ub = u_all[l].reshape(n_tok, model)
            for n in range(ff // fc):
                sl = slice(n * fc, (n + 1) * fc)
                one = jnp.dot(ub, w1_s[i, :, sl], preferred_element_type=F32)
                three = jnp.dot(ub, w3_s[i, :, sl], preferred_element_type=F32)
                inner_s[i, :, sl] = (jax.nn.silu(one) * three).astype(BF16)

    def gate_columns(l):
        gates = g_all[l].reshape(n_tok, 128)
        lane = lax.broadcasted_iota(jnp.int32, (n_tok, 128), 1)
        first = (ep * n_pool + p) * n_loc
        for i in range(n_loc):
            g = jnp.sum(jnp.where(lane == first + i, gates, 0.0), axis=-1, keepdims=True)
            gb_s[i] = jnp.broadcast_to(g, (n_tok, 128))

    def down_block(l, n):
        acc = [jnp.zeros((n_tok, 128), F32) for _ in range(cw // 128)]
        for i in range(n_loc):
            y = jnp.dot(inner_s[i], w2_s[n, i], preferred_element_type=F32).astype(BF16).astype(F32)
            g = gb_s[i]
            for b in range(cw // 128):
                acc[b] = acc[b] + jnp.where(g > 0.0, g * y[:, b * 128:(b + 1) * 128], 0.0)
        for b in range(cw // 128):
            part[l, n, :, :, b * 128:(b + 1) * 128] = acc[b].reshape(n_dev, tok, 128)

    def forward_chunk(l, n):
        for k in far_first:
            d_copy(l, n, k).wait_recv()
            red[l, n, k] = part[l, n, peer(*chips[k], 1)[0]] + sbuf[l, n, k]
            c_copy(l, n, k).start()

    def experts(l):
        with jax.named_scope(f"uwait{l}"):
            for j in range(len(others)):
                u_copy(l, j, peer(*others[j])[0]).wait_recv()
        for g in range(n_loc // per):
            with jax.named_scope(f"up{l}"):
                up_block(l, g)
            if l + 1 < layers:
                start_up(l + 1, g * per, (g + 1) * per)
            if g == 0:
                with jax.named_scope(f"gwait{l}"):
                    for j in range(len(others)):
                        g_copy(l, j, peer(*others[j])[0]).wait_recv()
                gate_columns(l)
        for n in range(n_chunk):
            with jax.named_scope(f"downwait{l}"):
                down_copy(l, n).wait()
            with jax.named_scope(f"down{l}"):
                down_block(l, n)
            for k in far_first + (0,):
                d_copy(l, n, k).start()
            if l + 1 < layers:
                down_copy(l + 1, n).start()
            if n > 0:
                with jax.named_scope(f"fwd{l}"):
                    forward_chunk(l, n - 1)
        with jax.named_scope(f"fwd{l}"):
            forward_chunk(l, n_chunk - 1)

    other = 1 - p
    orow = pl.multiple_of(other * tok, tok)

    def x_copy(n, row):
        view = xfin.at[pl.ds(row, tok), pl.ds(n * cw, cw)]
        return pltpu.make_async_remote_copy(
            src_ref=view, dst_ref=view, send_sem=sem_x.at[0, n], recv_sem=sem_x.at[1, n],
            device_id={"pool": other, "ep": ep}, device_id_type=MESH)

    def combine(l):
        for n in range(n_chunk):
            d_copy(l, n, 0).wait_recv()
            total = part[l, n, me] + sbuf[l, n, 0]
            for k in far_first:
                c_copy(l, n, k).wait_recv()
                total = total + rbuf[l, n, k]
            sl = slice(n * cw, (n + 1) * cw)
            x = (a_s[:, sl] + total).astype(BF16)
            if l + 1 < layers:
                x_s[:, sl] = x.astype(F32)
            else:
                xfin[pl.ds(row0, tok), sl] = x
                x_copy(n, row0).start()

    for l in range(layers):
        with jax.named_scope(f"attention{l}"):
            attention(l)
        if l == 0:
            with jax.named_scope("barrier"):
                pl.semaphore_wait(barrier, len(others))
        with jax.named_scope(f"route{l}"):
            route(l)
        if l + 1 < layers:
            for k in range(7):
                attn_copy(l + 1, k).start()
        experts(l)
        with jax.named_scope(f"combine{l}"):
            combine(l)

    with jax.named_scope("xwait"):
        for n in range(n_chunk):
            x_copy(n, orow).wait_recv()
    with jax.named_scope("drain"):
        for n in range(n_chunk):
            x_copy(n, row0).wait_send()
        for l in range(layers):
            for j in range(len(others)):
                u_copy(l, j, me).wait_send()
                g_copy(l, j, me).wait_send()
            for n in range(n_chunk):
                for k in range(4):
                    d_copy(l, n, k).wait_send()
                    if k:
                        c_copy(l, n, k).wait_send()


def solution(mesh):
    n_pool = mesh.shape["pool"]
    n_ep = mesh.shape["ep"]
    n_dev = n_pool * n_ep

    def body(hidden, k_cache, v_cache, lengths, expert_ids, w_query, w_key, w_value, w_out, w_router, w_gate, w_up, w_down):
        layers, n_tok, seq, kvh, hd = k_cache.shape
        tok = n_tok // n_pool
        model = hidden.shape[1]
        heads = w_query.shape[2] // hd
        n_loc = w_gate.shape[1] // n_pool
        ff = w_gate.shape[3]
        n_exp = w_router.shape[2]
        topk = expert_ids.shape[2]
        cw = 256
        n_chunk = model // cw
        kflat = k_cache.reshape(layers, n_tok, seq * kvh, hd)
        vflat = v_cache.reshape(layers, n_tok, seq * kvh, hd)
        ids = jnp.swapaxes(expert_ids, 1, 2)
        router = jnp.swapaxes(w_router, 1, 2)
        cfg = (layers, n_pool, n_ep, tok, heads, kvh, hd, seq, n_loc, ff, model)
        any_spec = pl.BlockSpec(memory_space=pl.ANY)
        smem_spec = pl.BlockSpec(memory_space=pltpu.SMEM)
        vm = pltpu.VMEM
        dma = pltpu.SemaphoreType.DMA
        return pl.pallas_call(
            functools.partial(kernel, cfg),
            out_shape=vm((n_tok, model), BF16),
            in_specs=[any_spec] * 3 + [smem_spec] + [any_spec] * 9,
            out_specs=pl.BlockSpec(memory_space=pltpu.VMEM),
            scratch_shapes=[
                vm((model, heads * hd), BF16), vm((model, kvh * hd), BF16), vm((model, kvh * hd), BF16),
                vm((heads * hd, model), BF16), vm((n_exp, model), F32),
                vm((tok, seq * kvh, hd), BF16), vm((tok, seq * kvh, hd), BF16),
                vm((n_loc, model, ff), BF16), vm((n_loc, model, ff), BF16), vm((n_chunk, n_loc, ff, cw), BF16),
                vm((tok, model), F32), vm((tok, model), F32), vm((layers, topk, n_tok), jnp.int32), vm((layers, 128, topk), F32),
                vm((heads * tok, hd), F32), vm((kvh * seq // 128, heads * tok, 128), F32), vm((heads * tok, hd), F32),
                vm((layers, n_dev, tok, model), BF16), vm((layers, n_dev, tok, 128), F32), vm((n_loc, n_dev * tok, 128), F32),
                vm((n_loc, n_dev * tok, ff), BF16), vm((layers, n_chunk, n_dev, tok, cw), F32),
                vm((layers, n_chunk, 4, tok, cw), F32), vm((layers, n_chunk, 4, tok, cw), F32), vm((layers, n_chunk, 4, tok, cw), F32),
                vm((tok, model), BF16),
                dma((9,)), dma((2, n_loc)), dma((n_chunk,)), dma((layers, 7)), dma((layers, 7)), dma((layers, 7)), dma((layers, 7)),
                dma((layers, n_chunk, 4)), dma((layers, n_chunk, 4)), dma((layers, n_chunk, 4)), dma((layers, n_chunk, 4)), dma((2, n_chunk)),
            ],
            compiler_params=pltpu.CompilerParams(
                collective_id=0, has_side_effects=True, vmem_limit_bytes=63 * 1024 * 1024),
        )(hidden, kflat, vflat, lengths, ids, w_query, w_key, w_value, w_out, router, w_gate, w_up, w_down)

    rows_spec = ("dp", "ep")
    in_specs = (P(rows_spec, None), P(None, rows_spec), P(None, rows_spec), P(rows_spec), P(None, rows_spec, None), P(), P(), P(), P(), P(), P(None, "ep"), P(None, "ep"), P(None, "ep"))
    return jax.shard_map(body, mesh=mesh, in_specs=in_specs, out_specs=P(rows_spec, None), check_vma=False)
```

time: 63.4 us -> 49.6 us (0.78)
  Pallas kernels: 61.8 us -> 48.9 us
  local copies, waits for them, and re-layouts: 1.47 us -> 0.63 us
    pallas_call x1, Pallas kernels: 61.8 us -> 48.9 us  [body(): pl.pallas_call(functools.partial(kernel, cfg), out_shape=vm((n_tok, model...]
    unnamed x1, local copies, waits for them, and re-layouts: 1.47 us -> 0.63 us
where the time goes in v1:
time: 49.6 us; the launch traced here: 49.5 us
  Pallas kernels  48.9 us (99%)
  local copies, waits for them, and re-layouts  0.63 us (1%)
    pallas_call x1, Pallas kernels, body(): pl.pallas_call(functools.partial(kernel, cfg), out_shape=vm((n_tok, model...  48.9 us

profile of v1, /device:TPU:0, one launch (start us, length us, event | category | flops | bytes accessed | tf_op | source)
XLA Modules:
  0.0 49.5 jit_solution(4842142668031870883)
XLA Ops:
  0.0 48.9 %shard_map.127 = bf16[32,1024]{1,0:T(8,128)(2,1)S(1)} custom-call(bf16[32,1024]{1,0:T(8,128)(2,1)} %hid.1, bf16[2,32,256,128]{3,2,1,0:T(8,128)(2,1)} %bitcast.4, bf16[2,32,256,128]{3,2,1,0:T(8,128)(2,1)} %bitcast.5, s32[32]{0:T(128)} %lens.1, s32[2,8,32]{2,1,0:T(8,128)} %bitcast.7, bf16[2,1024,2048]{2,1,0:T(8,128)(2,1)} %wq.1, bf16[2,1024,256]{2,1,0:T(8,128)(2,1)} %wk.1, ...), custom_call_target="tpu_custom_call" | custom-call | tf_op jit(solution)/shard_map/pallas_call | solution.py:379
  48.9 0.6 %copy.15 = bf16[32,1024]{1,0:T(8,128)(2,1)} copy(bf16[32,1024]{1,0:T(8,128)(2,1)S(1)} %shard_map.127) | data formatting | bytes 131072

commit v2 on v1

--- a/solution.py
+++ b/solution.py
@@ -23,7 +23,7 @@
 def kernel(cfg, hid, kc, vc, lens, ids, wq, wk, wv, wo, wr, wg, wu, wd, xfin,
            wq_s, wk_s, wv_s, wo_s, wr_s, kb, vb, w1_s, w3_s, w2_s,
            x_s, a_s, ids_s, idt_s, q_s, s_s, o_s,
-           u_all, g_all, gb_s, inner_s, part, sbuf, red, rbuf, hid_s,
+           u_all, g_all, gb_s, inner_s, part, sbuf, red, rbuf, hid_s, lens_s,
            sem_a, sem_w, sem_w2, sem_u, sem_us, sem_g, sem_gs, sem_d, sem_ds, sem_c, sem_cs, sem_x):
     layers, n_pool, n_ep, tok, heads, kvh, hd, seq, n_loc, ff, model = cfg
     n_dev = n_pool * n_ep
@@ -43,10 +43,6 @@
     others = [(1, 1, 1), (1, 1, 0), (0, 1, 1), (1, 0, 1), (0, 1, 0), (1, 0, 0), (0, 0, 1)]
     chips = [(0, 0), (0, 1), (1, 0), (1, 1)]
 
-    barrier = pltpu.get_barrier_semaphore()
-    for rel in others:
-        pl.semaphore_signal(barrier, inc=1, device_id=peer(*rel)[1], device_id_type=MESH)
-
     def attn_copy(l, k):
         src, dst = [
             (lambda: wq.at[l], wq_s), (lambda: wk.at[l], wk_s), (lambda: wv.at[l], wv_s),
@@ -55,12 +51,16 @@
         ][k]
         return pltpu.make_async_copy(src(), dst, sem_a.at[k])
 
-    def up_copies(l, i):
-        e = p * n_loc + i
+    def up_copies(l, g):
+        e = p * n_loc + g * 2
         return [
-            pltpu.make_async_copy(wg.at[l, e], w1_s.at[i], sem_w.at[0, i]),
-            pltpu.make_async_copy(wu.at[l, e], w3_s.at[i], sem_w.at[1, i]),
+            pltpu.make_async_copy(wg.at[l, pl.ds(e, 2)], w1_s.at[pl.ds(g * 2, 2)], sem_w.at[0, g]),
+            pltpu.make_async_copy(wu.at[l, pl.ds(e, 2)], w3_s.at[pl.ds(g * 2, 2)], sem_w.at[1, g]),
         ]
+
+    def start_up(l, g):
+        for c in up_copies(l, g):
+            c.start()
 
     def down_copy(l, n):
         return pltpu.make_async_copy(
@@ -68,21 +68,24 @@
 
     hid_copy = pltpu.make_async_copy(hid.at[pl.ds(row0, tok)], hid_s, sem_a.at[7])
     ids_copy = pltpu.make_async_copy(ids, ids_s, sem_a.at[8])
+    len_copy = pltpu.make_async_copy(lens, lens_s, sem_a.at[9])
+    len_copy.start()
     hid_copy.start()
     ids_copy.start()
-    for k in range(7):
+    for k in range(3):
         attn_copy(0, k).start()
 
-    def start_up(l, lo, hi):
-        for i in range(lo, hi):
-            for c in up_copies(l, i):
-                c.start()
-
+    barrier = pltpu.get_barrier_semaphore()
+    for rel in others:
+        pl.semaphore_signal(barrier, inc=1, device_id=peer(*rel)[1], device_id_type=MESH)
+
+    with jax.named_scope("lenwait"):
+        len_copy.wait()
     rows = lax.broadcasted_iota(jnp.int32, (tok, hd), 0)
     lanes = lax.broadcasted_iota(jnp.int32, (tok, hd), 1)
     len_i = jnp.zeros((tok, hd), jnp.int32)
     for t in range(tok):
-        len_i = jnp.where(rows == t, lens[p * tok + t], len_i)
+        len_i = jnp.where(rows == t, lens_s[p * tok + t], len_i)
     half = hd // 2
     pair = jnp.where(lanes < half, lanes, lanes - half).astype(F32)
     freq = jnp.exp(pair * (-2.0 * math.log(ROPE_BASE) / hd))
@@ -99,6 +102,8 @@
     for l in range(layers):
         idf = jnp.concatenate([ids_s[l].astype(F32), jnp.zeros((ids_s.shape[1], 128 - ids_s.shape[2]), F32)], axis=1)
         idt_s[l] = jnp.transpose(idf)
+    for k in range(3, 7):
+        attn_copy(0, k).start()
     with jax.named_scope("hidwait"):
         hid_copy.wait()
     x_s[...] = hid_s[...].astype(F32)
@@ -113,7 +118,7 @@
             for k in range(3 if l == 0 else 7):
                 attn_copy(l, k).wait()
         if l == 0:
-            start_up(0, 0, 2)
+            start_up(0, 0)
         qc = 256
         for c in range(heads * hd // qc):
             qq = jnp.dot(h, wq_s[:, c * qc:(c + 1) * qc], preferred_element_type=F32)
@@ -128,7 +133,7 @@
             with jax.named_scope(f"await3_{l}"):
                 attn_copy(l, 3).wait()
                 attn_copy(l, 4).wait()
-            start_up(0, 2, 4)
+            start_up(0, 1)
         for t in range(tok):
             qt = q_s[pl.ds(t, heads, stride=tok), :].astype(BF16)
             st = lax.dot_general(qt, kb[t], NT, preferred_element_type=F32) * scale
@@ -167,33 +172,46 @@
         if l == 0:
             with jax.named_scope(f"await5_{l}"):
                 attn_copy(l, 5).wait()
-            start_up(0, 4, n_loc)
-            for n in range(n_chunk):
-                down_copy(0, n).start()
+            start_up(0, 2)
         oc = 256
         for c in range(model // oc):
             sl = slice(c * oc, (c + 1) * oc)
             a_s[:, sl] = (x[:, sl] + jnp.dot(o, wo_s[:, sl], preferred_element_type=F32)).astype(BF16).astype(F32)
 
-    def u_copy(l, j, src):
-        return pltpu.make_async_remote_copy(
-            src_ref=u_all.at[l, src], dst_ref=u_all.at[l, src], send_sem=sem_us.at[l, j], recv_sem=sem_u.at[l, j],
+    def u_copy(l, k):
+        view = u_all.at[l, me]
+        return pltpu.make_async_remote_copy(
+            src_ref=view, dst_ref=view, send_sem=sem_us.at[l], recv_sem=sem_u.at[l, k],
+            device_id=peer(*chips[k], 1)[1], device_id_type=MESH)
+
+    def u_relay(l, k):
+        view = u_all.at[l, peer(*chips[k], 1)[0]]
+        return pltpu.make_async_remote_copy(
+            src_ref=view, dst_ref=view, send_sem=sem_us.at[l], recv_sem=sem_u.at[l, 0],
+            device_id=peer(0, 0, 1)[1], device_id_type=MESH)
+
+    def u_arrival(l, k):
+        view = u_all.at[l, peer(*chips[k], 1)[0]]
+        return pltpu.make_async_copy(view, view, sem_u.at[l, k])
+
+    def g_copy(l, j):
+        view = g_all.at[l, me]
+        return pltpu.make_async_remote_copy(
+            src_ref=view, dst_ref=view, send_sem=sem_gs.at[l], recv_sem=sem_g.at[l],
             device_id=peer(*others[j])[1], device_id_type=MESH)
 
-    def g_copy(l, j, src):
-        return pltpu.make_async_remote_copy(
-            src_ref=g_all.at[l, src], dst_ref=g_all.at[l, src], send_sem=sem_gs.at[l, j], recv_sem=sem_g.at[l, j],
-            device_id=peer(*others[j])[1], device_id_type=MESH)
+    def wait_all(view, sem):
+        pltpu.make_async_copy(view, view, sem).wait()
 
     def d_copy(l, n, k):
         dest = peer(0, 0, 1)[0] if k == 0 else peer(*chips[k], 0)[0]
         return pltpu.make_async_remote_copy(
-            src_ref=part.at[l, n, dest], dst_ref=sbuf.at[l, n, k], send_sem=sem_ds.at[l, n, k], recv_sem=sem_d.at[l, n, k],
+            src_ref=part.at[l, n, dest], dst_ref=sbuf.at[l, n, k], send_sem=sem_ds.at[l], recv_sem=sem_d.at[l, n],
             device_id=peer(0, 0, 1)[1], device_id_type=MESH)
 
     def c_copy(l, n, k):
         return pltpu.make_async_remote_copy(
-            src_ref=red.at[l, n, k], dst_ref=rbuf.at[l, n, k], send_sem=sem_cs.at[l, n, k], recv_sem=sem_c.at[l, n, k],
+            src_ref=red.at[l, n, k], dst_ref=rbuf.at[l, n, k], send_sem=sem_cs.at[l], recv_sem=sem_c.at[l, n],
             device_id=peer(*chips[k], 1)[1], device_id_type=MESH)
 
     far_first = (3, 1, 2)
@@ -201,8 +219,8 @@
     def route(l):
         u = rms_normed(a_s[...]).astype(BF16)
         u_all[l, me] = u
-        for j in range(len(others)):
-            u_copy(l, j, me).start()
+        for k in far_first + (0,):
+            u_copy(l, k).start()
         if l == 0:
             with jax.named_scope(f"await6_{l}"):
                 attn_copy(l, 6).wait()
@@ -223,18 +241,13 @@
         gates = w / jnp.sum(w, axis=-1, keepdims=True)
         g_all[l, me] = jnp.concatenate([gates, jnp.zeros((tok, 128 - n_exp), F32)], axis=1)
         for j in range(len(others)):
-            g_copy(l, j, me).start()
+            g_copy(l, j).start()
 
     n_tok = n_dev * tok
     fc = 256
-    per = 4
-
-    def up_block(l, g):
-        with jax.named_scope(f"upwait{l}"):
-            for i in range(g * per, (g + 1) * per):
-                for c in up_copies(l, i):
-                    c.wait()
-        for i in range(g * per, (g + 1) * per):
+
+    def up_block(l, lo, hi):
+        for i in range(lo, hi):
             ub = u_all[l].reshape(n_tok, model)
             for n in range(ff // fc):
                 sl = slice(n * fc, (n + 1) * fc)
@@ -261,37 +274,62 @@
             part[l, n, :, :, b * 128:(b + 1) * 128] = acc[b].reshape(n_dev, tok, 128)
 
     def forward_chunk(l, n):
+        wait_all(sbuf.at[l, n], sem_d.at[l, n])
         for k in far_first:
-            d_copy(l, n, k).wait_recv()
             red[l, n, k] = part[l, n, peer(*chips[k], 1)[0]] + sbuf[l, n, k]
             c_copy(l, n, k).start()
 
+    def up_wait(l, g):
+        with jax.named_scope(f"upwait{l}"):
+            for c in up_copies(l, g):
+                c.wait()
+
     def experts(l):
         with jax.named_scope(f"uwait{l}"):
-            for j in range(len(others)):
-                u_copy(l, j, peer(*others[j])[0]).wait_recv()
-        for g in range(n_loc // per):
+            for k in (2, 3, 1):
+                u_arrival(l, k).wait()
+                u_relay(l, k).start()
+        with jax.named_scope(f"urelay{l}"):
+            wait_all(u_all.at[l, pl.ds(0, 4)], sem_u.at[l, 0])
+        n_pair = n_loc // 2
+        step = 1 if l == 0 else 2
+        if l > 0:
+            down_copy(l, 0).start()
+            down_copy(l, 1).start()
+        for g in range(0, n_pair, step):
+            for s in range(step):
+                up_wait(l, g + s)
+            if l == 0 and g > 0:
+                down_copy(l, g - 1).start()
+            if l > 0 and g > 0:
+                down_copy(l, 2).start()
+                down_copy(l, 3).start()
             with jax.named_scope(f"up{l}"):
-                up_block(l, g)
-            if l + 1 < layers:
-                start_up(l + 1, g * per, (g + 1) * per)
+                up_block(l, g * 2, (g + step) * 2)
             if g == 0:
                 with jax.named_scope(f"gwait{l}"):
-                    for j in range(len(others)):
-                        g_copy(l, j, peer(*others[j])[0]).wait_recv()
+                    wait_all(g_all.at[l, pl.ds(0, len(others))], sem_g.at[l])
                 gate_columns(l)
+        if l == 0:
+            down_copy(l, n_chunk - 1).start()
         for n in range(n_chunk):
             with jax.named_scope(f"downwait{l}"):
                 down_copy(l, n).wait()
+            if l + 1 < layers:
+                if n == 0:
+                    for k in range(7):
+                        attn_copy(l + 1, k).start()
+                else:
+                    start_up(l + 1, n - 1)
             with jax.named_scope(f"down{l}"):
                 down_block(l, n)
             for k in far_first + (0,):
                 d_copy(l, n, k).start()
-            if l + 1 < layers:
-                down_copy(l + 1, n).start()
             if n > 0:
                 with jax.named_scope(f"fwd{l}"):
                     forward_chunk(l, n - 1)
+        if l + 1 < layers:
+            start_up(l + 1, n_pair - 1)
         with jax.named_scope(f"fwd{l}"):
             forward_chunk(l, n_chunk - 1)
 
@@ -301,15 +339,14 @@
     def x_copy(n, row):
         view = xfin.at[pl.ds(row, tok), pl.ds(n * cw, cw)]
         return pltpu.make_async_remote_copy(
-            src_ref=view, dst_ref=view, send_sem=sem_x.at[0, n], recv_sem=sem_x.at[1, n],
+            src_ref=view, dst_ref=view, send_sem=sem_x.at[0], recv_sem=sem_x.at[1],
             device_id={"pool": other, "ep": ep}, device_id_type=MESH)
 
     def combine(l):
         for n in range(n_chunk):
-            d_copy(l, n, 0).wait_recv()
             total = part[l, n, me] + sbuf[l, n, 0]
+            wait_all(rbuf.at[l, n, pl.ds(1, 3)], sem_c.at[l, n])
             for k in far_first:
-                c_copy(l, n, k).wait_recv()
                 total = total + rbuf[l, n, k]
             sl = slice(n * cw, (n + 1) * cw)
             x = (a_s[:, sl] + total).astype(BF16)
@@ -327,28 +364,21 @@
                 pl.semaphore_wait(barrier, len(others))
         with jax.named_scope(f"route{l}"):
             route(l)
-        if l + 1 < layers:
-            for k in range(7):
-                attn_copy(l + 1, k).start()
+        if l == 0:
+            start_up(0, 3)
         experts(l)
         with jax.named_scope(f"combine{l}"):
             combine(l)
 
     with jax.named_scope("xwait"):
-        for n in range(n_chunk):
-            x_copy(n, orow).wait_recv()
+        wait_all(xfin.at[pl.ds(orow, tok)], sem_x.at[1])
     with jax.named_scope("drain"):
-        for n in range(n_chunk):
-            x_copy(n, row0).wait_send()
+        wait_all(xfin.at[pl.ds(row0, tok)], sem_x.at[0])
         for l in range(layers):
-            for j in range(len(others)):
-                u_copy(l, j, me).wait_send()
-                g_copy(l, j, me).wait_send()
-            for n in range(n_chunk):
-                for k in range(4):
-                    d_copy(l, n, k).wait_send()
-                    if k:
-                        c_copy(l, n, k).wait_send()
+            wait_all(u_all.at[l, pl.ds(0, 7)], sem_us.at[l])
+            wait_all(g_all.at[l, pl.ds(0, 7)], sem_gs.at[l])
+            wait_all(part.at[l, pl.ds(0, n_chunk // 2)], sem_ds.at[l])
+            wait_all(red.at[l, :, pl.ds(1, 3)], sem_cs.at[l])
 
 
 def solution(mesh):
@@ -373,13 +403,12 @@
         router = jnp.swapaxes(w_router, 1, 2)
         cfg = (layers, n_pool, n_ep, tok, heads, kvh, hd, seq, n_loc, ff, model)
         any_spec = pl.BlockSpec(memory_space=pl.ANY)
-        smem_spec = pl.BlockSpec(memory_space=pltpu.SMEM)
         vm = pltpu.VMEM
         dma = pltpu.SemaphoreType.DMA
         return pl.pallas_call(
             functools.partial(kernel, cfg),
             out_shape=vm((n_tok, model), BF16),
-            in_specs=[any_spec] * 3 + [smem_spec] + [any_spec] * 9,
+            in_specs=[any_spec] * 13,
             out_specs=pl.BlockSpec(memory_space=pltpu.VMEM),
             scratch_shapes=[
                 vm((model, heads * hd), BF16), vm((model, kvh * hd), BF16), vm((model, kvh * hd), BF16),
@@ -391,9 +420,9 @@
                 vm((layers, n_dev, tok, model), BF16), vm((layers, n_dev, tok, 128), F32), vm((n_loc, n_dev * tok, 128), F32),
                 vm((n_loc, n_dev * tok, ff), BF16), vm((layers, n_chunk, n_dev, tok, cw), F32),
                 vm((layers, n_chunk, 4, tok, cw), F32), vm((layers, n_chunk, 4, tok, cw), F32), vm((layers, n_chunk, 4, tok, cw), F32),
-                vm((tok, model), BF16),
-                dma((9,)), dma((2, n_loc)), dma((n_chunk,)), dma((layers, 7)), dma((layers, 7)), dma((layers, 7)), dma((layers, 7)),
-                dma((layers, n_chunk, 4)), dma((layers, n_chunk, 4)), dma((layers, n_chunk, 4)), dma((layers, n_chunk, 4)), dma((2, n_chunk)),
+                vm((tok, model), BF16), pltpu.SMEM((n_tok,), jnp.int32),
+                dma((10,)), dma((2, n_loc // 2)), dma((n_chunk,)), dma((layers, 4)), dma((layers,)), dma((layers,)), dma((layers,)),
+                dma((layers, n_chunk)), dma((layers,)), dma((layers, n_chunk)), dma((layers,)), dma((2,)),
             ],
             compiler_params=pltpu.CompilerParams(
                 collective_id=0, has_side_effects=True, vmem_limit_bytes=63 * 1024 * 1024),

time: 49.6 us -> 44.7 us (0.901)
  Pallas kernels: 48.9 us -> 43.9 us
    pallas_call x1, Pallas kernels: 48.9 us -> 43.9 us  [body(): pl.pallas_call(functools.partial(kernel, cfg), out_shape=vm((n_tok, model...]
where the time goes in v2:
time: 44.7 us; the launch traced here: 44.6 us
  Pallas kernels  43.9 us (98%)
  local copies, waits for them, and re-layouts  0.63 us (1%)
    pallas_call x1, Pallas kernels, body(): pl.pallas_call(functools.partial(kernel, cfg), out_shape=vm((n_tok, model...  43.9 us

profile of v2, /device:TPU:0, one launch (start us, length us, event | category | flops | bytes accessed | tf_op | source)
XLA Modules:
  0.0 44.6 jit_solution(10116192322379614071)
XLA Ops:
  0.0 43.9 %shard_map.127 = bf16[32,1024]{1,0:T(8,128)(2,1)S(1)} custom-call(bf16[32,1024]{1,0:T(8,128)(2,1)} %hid.1, bf16[2,32,256,128]{3,2,1,0:T(8,128)(2,1)} %bitcast.4, bf16[2,32,256,128]{3,2,1,0:T(8,128)(2,1)} %bitcast.5, s32[32]{0:T(128)} %lens.1, s32[2,8,32]{2,1,0:T(8,128)} %bitcast.7, bf16[2,1024,2048]{2,1,0:T(8,128)(2,1)} %wq.1, bf16[2,1024,256]{2,1,0:T(8,128)(2,1)} %wk.1, ...), custom_call_target="tpu_custom_call" | custom-call | tf_op jit(solution)/shard_map/pallas_call | solution.py:408
  44.0 0.6 %copy.15 = bf16[32,1024]{1,0:T(8,128)(2,1)} copy(bf16[32,1024]{1,0:T(8,128)(2,1)S(1)} %shard_map.127) | data formatting | bytes 131072

commit v3 on v2

--- a/solution.py
+++ b/solution.py
@@ -23,11 +23,12 @@
 def kernel(cfg, hid, kc, vc, lens, ids, wq, wk, wv, wo, wr, wg, wu, wd, xfin,
            wq_s, wk_s, wv_s, wo_s, wr_s, kb, vb, w1_s, w3_s, w2_s,
            x_s, a_s, ids_s, idt_s, q_s, s_s, o_s,
-           u_all, g_all, gb_s, inner_s, part, sbuf, red, rbuf, hid_s, lens_s,
+           u_all, g_all, gb_s, inner_s, part, sbuf, red, rbuf, sbuf2, red2, rbuf2, abuf, hid_s, lens_s,
            sem_a, sem_w, sem_w2, sem_u, sem_us, sem_g, sem_gs, sem_d, sem_ds, sem_c, sem_cs, sem_x):
     layers, n_pool, n_ep, tok, heads, kvh, hd, seq, n_loc, ff, model = cfg
     n_dev = n_pool * n_ep
     n_chunk, _, _, cw = w2_s.shape
+    n_both = sbuf2.shape[0]
     p = lax.axis_index("pool")
     ep = lax.axis_index("ep")
     me = p * n_ep + ep
@@ -117,8 +118,6 @@
         with jax.named_scope(f"await0_{l}"):
             for k in range(3 if l == 0 else 7):
                 attn_copy(l, k).wait()
-        if l == 0:
-            start_up(0, 0)
         qc = 256
         for c in range(heads * hd // qc):
             qq = jnp.dot(h, wq_s[:, c * qc:(c + 1) * qc], preferred_element_type=F32)
@@ -133,7 +132,7 @@
             with jax.named_scope(f"await3_{l}"):
                 attn_copy(l, 3).wait()
                 attn_copy(l, 4).wait()
-            start_up(0, 1)
+            start_up(0, 0)
         for t in range(tok):
             qt = q_s[pl.ds(t, heads, stride=tok), :].astype(BF16)
             st = lax.dot_general(qt, kb[t], NT, preferred_element_type=F32) * scale
@@ -172,6 +171,7 @@
         if l == 0:
             with jax.named_scope(f"await5_{l}"):
                 attn_copy(l, 5).wait()
+            start_up(0, 1)
             start_up(0, 2)
         oc = 256
         for c in range(model // oc):
@@ -181,23 +181,23 @@
     def u_copy(l, k):
         view = u_all.at[l, me]
         return pltpu.make_async_remote_copy(
-            src_ref=view, dst_ref=view, send_sem=sem_us.at[l], recv_sem=sem_u.at[l, k],
+            src_ref=view, dst_ref=view, send_sem=sem_us.at[0], recv_sem=sem_u.at[k],
             device_id=peer(*chips[k], 1)[1], device_id_type=MESH)
 
     def u_relay(l, k):
         view = u_all.at[l, peer(*chips[k], 1)[0]]
         return pltpu.make_async_remote_copy(
-            src_ref=view, dst_ref=view, send_sem=sem_us.at[l], recv_sem=sem_u.at[l, 0],
+            src_ref=view, dst_ref=view, send_sem=sem_us.at[0], recv_sem=sem_u.at[0],
             device_id=peer(0, 0, 1)[1], device_id_type=MESH)
 
     def u_arrival(l, k):
         view = u_all.at[l, peer(*chips[k], 1)[0]]
-        return pltpu.make_async_copy(view, view, sem_u.at[l, k])
+        return pltpu.make_async_copy(view, view, sem_u.at[k])
 
     def g_copy(l, j):
         view = g_all.at[l, me]
         return pltpu.make_async_remote_copy(
-            src_ref=view, dst_ref=view, send_sem=sem_gs.at[l], recv_sem=sem_g.at[l],
+            src_ref=view, dst_ref=view, send_sem=sem_gs.at[0], recv_sem=sem_g.at[0],
             device_id=peer(*others[j])[1], device_id_type=MESH)
 
     def wait_all(view, sem):
@@ -206,12 +206,12 @@
     def d_copy(l, n, k):
         dest = peer(0, 0, 1)[0] if k == 0 else peer(*chips[k], 0)[0]
         return pltpu.make_async_remote_copy(
-            src_ref=part.at[l, n, dest], dst_ref=sbuf.at[l, n, k], send_sem=sem_ds.at[l], recv_sem=sem_d.at[l, n],
+            src_ref=part.at[l, n, dest], dst_ref=sbuf.at[l, n, k], send_sem=sem_ds.at[0], recv_sem=sem_d.at[n],
             device_id=peer(0, 0, 1)[1], device_id_type=MESH)
 
     def c_copy(l, n, k):
         return pltpu.make_async_remote_copy(
-            src_ref=red.at[l, n, k], dst_ref=rbuf.at[l, n, k], send_sem=sem_cs.at[l], recv_sem=sem_c.at[l, n],
+            src_ref=red.at[l, n, k], dst_ref=rbuf.at[l, n, k], send_sem=sem_cs.at[0], recv_sem=sem_c.at[n],
             device_id=peer(*chips[k], 1)[1], device_id_type=MESH)
 
     far_first = (3, 1, 2)
@@ -257,11 +257,10 @@
 
     def gate_columns(l):
         gates = g_all[l].reshape(n_tok, 128)
-        lane = lax.broadcasted_iota(jnp.int32, (n_tok, 128), 1)
         first = (ep * n_pool + p) * n_loc
+        gates = pltpu.roll(gates, lax.rem(128 - first, 128), 1)
         for i in range(n_loc):
-            g = jnp.sum(jnp.where(lane == first + i, gates, 0.0), axis=-1, keepdims=True)
-            gb_s[i] = jnp.broadcast_to(g, (n_tok, 128))
+            gb_s[i] = jnp.broadcast_to(gates[:, i:i + 1], (n_tok, 128))
 
     def down_block(l, n):
         acc = [jnp.zeros((n_tok, 128), F32) for _ in range(cw // 128)]
@@ -273,8 +272,43 @@
         for b in range(cw // 128):
             part[l, n, :, :, b * 128:(b + 1) * 128] = acc[b].reshape(n_dev, tok, 128)
 
+    def both(l, n):
+        return l == layers - 1 and n >= n_chunk - n_both
+
+    def d2_copy(l, n, k):
+        dest = peer(*chips[k], 0)[0] if k < 4 else peer(*chips[(k - 4) * 2], 1)[0]
+        return pltpu.make_async_remote_copy(
+            src_ref=part.at[l, n, dest], dst_ref=sbuf2.at[n - n_chunk + n_both, k], send_sem=sem_ds.at[1], recv_sem=sem_d.at[n],
+            device_id=peer(0, 0, 1)[1], device_id_type=MESH)
+
+    def c2_copy(n, k, r):
+        m = n - n_chunk + n_both
+        return pltpu.make_async_remote_copy(
+            src_ref=red2.at[m, (k + 2 * r) % 4], dst_ref=rbuf2.at[m, k, r], send_sem=sem_cs.at[1], recv_sem=sem_c.at[n],
+            device_id=peer(*chips[k], 1)[1], device_id_type=MESH)
+
+    def share_chunk(l, n):
+        if both(l, n):
+            for k in (3, 1, 2, 0, 4, 5):
+                d2_copy(l, n, k).start()
+        else:
+            for k in far_first + (0,):
+                d_copy(l, n, k).start()
+
     def forward_chunk(l, n):
-        wait_all(sbuf.at[l, n], sem_d.at[l, n])
+        if both(l, n):
+            m = n - n_chunk + n_both
+            wait_all(sbuf2.at[m], sem_d.at[n])
+            for k in (3, 1, 2, 0):
+                red2[m, k] = part[l, n, peer(*chips[k], 1)[0]] + sbuf2[m, k]
+                if k == 1:
+                    for q in (3, 1):
+                        for r in range(2):
+                            c2_copy(n, q, r).start()
+            for r in range(2):
+                c2_copy(n, 2, r).start()
+            return
+        wait_all(sbuf.at[l, n], sem_d.at[n])
         for k in far_first:
             red[l, n, k] = part[l, n, peer(*chips[k], 1)[0]] + sbuf[l, n, k]
             c_copy(l, n, k).start()
@@ -290,28 +324,29 @@
                 u_arrival(l, k).wait()
                 u_relay(l, k).start()
         with jax.named_scope(f"urelay{l}"):
-            wait_all(u_all.at[l, pl.ds(0, 4)], sem_u.at[l, 0])
+            wait_all(u_all.at[l, pl.ds(0, 4)], sem_u.at[0])
         n_pair = n_loc // 2
-        step = 1 if l == 0 else 2
         if l > 0:
             down_copy(l, 0).start()
             down_copy(l, 1).start()
-        for g in range(0, n_pair, step):
-            for s in range(step):
-                up_wait(l, g + s)
-            if l == 0 and g > 0:
-                down_copy(l, g - 1).start()
-            if l > 0 and g > 0:
-                down_copy(l, 2).start()
-                down_copy(l, 3).start()
+        blocks = (2, 2) if l == 0 else (4,)
+        lo = 0
+        for gi, step in enumerate(blocks):
+            for g in range(lo, lo + step):
+                up_wait(l, g)
+            if gi == len(blocks) - 1:
+                for n in range(2, n_chunk):
+                    down_copy(l, n).start()
+            elif l == 0:
+                for n in range(2):
+                    down_copy(l, n).start()
+            if gi == 0:
+                wait_all(g_all.at[l, pl.ds(0, len(others))], sem_g.at[0])
             with jax.named_scope(f"up{l}"):
-                up_block(l, g * 2, (g + step) * 2)
-            if g == 0:
-                with jax.named_scope(f"gwait{l}"):
-                    wait_all(g_all.at[l, pl.ds(0, len(others))], sem_g.at[l])
-                gate_columns(l)
-        if l == 0:
-            down_copy(l, n_chunk - 1).start()
+                up_block(l, lo * 2, (lo + step) * 2)
+                if gi == 0:
+                    gate_columns(l)
+            lo += step
         for n in range(n_chunk):
             with jax.named_scope(f"downwait{l}"):
                 down_copy(l, n).wait()
@@ -323,8 +358,7 @@
                     start_up(l + 1, n - 1)
             with jax.named_scope(f"down{l}"):
                 down_block(l, n)
-            for k in far_first + (0,):
-                d_copy(l, n, k).start()
+            share_chunk(l, n)
             if n > 0:
                 with jax.named_scope(f"fwd{l}"):
                     forward_chunk(l, n - 1)
@@ -342,13 +376,28 @@
             src_ref=view, dst_ref=view, send_sem=sem_x.at[0], recv_sem=sem_x.at[1],
             device_id={"pool": other, "ep": ep}, device_id_type=MESH)
 
+    def a_copy():
+        return pltpu.make_async_remote_copy(
+            src_ref=abuf.at[0], dst_ref=abuf.at[1], send_sem=sem_x.at[2], recv_sem=sem_x.at[3],
+            device_id={"pool": other, "ep": ep}, device_id_type=MESH)
+
     def combine(l):
         for n in range(n_chunk):
+            sl = slice(n * cw, (n + 1) * cw)
+            if both(l, n):
+                m = n - n_chunk + n_both
+                if m == 0:
+                    a_copy().wait_recv()
+                wait_all(rbuf2.at[m, pl.ds(1, 3)], sem_c.at[n])
+                ac = slice(m * cw, (m + 1) * cw)
+                for r in range(2):
+                    total = part[l, n, peer(*chips[2 * r], 0)[0]] + sbuf2[m, 4 + r]
+                    total = (total + rbuf2[m, 2, r]) + (rbuf2[m, 1, r] + rbuf2[m, 3, r])
+                    xfin[pl.ds(orow if r else row0, tok), sl] = (abuf[r, :, ac].astype(F32) + total).astype(BF16)
+                continue
             total = part[l, n, me] + sbuf[l, n, 0]
-            wait_all(rbuf.at[l, n, pl.ds(1, 3)], sem_c.at[l, n])
-            for k in far_first:
-                total = total + rbuf[l, n, k]
-            sl = slice(n * cw, (n + 1) * cw)
+            wait_all(rbuf.at[l, n, pl.ds(1, 3)], sem_c.at[n])
+            total = (total + rbuf[l, n, 2]) + (rbuf[l, n, 1] + rbuf[l, n, 3])
             x = (a_s[:, sl] + total).astype(BF16)
             if l + 1 < layers:
                 x_s[:, sl] = x.astype(F32)
@@ -366,19 +415,24 @@
             route(l)
         if l == 0:
             start_up(0, 3)
+        if l == layers - 1:
+            abuf[0] = a_s[:, model - n_both * cw:].astype(BF16)
+            a_copy().start()
         experts(l)
         with jax.named_scope(f"combine{l}"):
             combine(l)
 
     with jax.named_scope("xwait"):
-        wait_all(xfin.at[pl.ds(orow, tok)], sem_x.at[1])
+        wait_all(xfin.at[pl.ds(orow, tok), pl.ds(0, model - n_both * cw)], sem_x.at[1])
     with jax.named_scope("drain"):
-        wait_all(xfin.at[pl.ds(row0, tok)], sem_x.at[0])
-        for l in range(layers):
-            wait_all(u_all.at[l, pl.ds(0, 7)], sem_us.at[l])
-            wait_all(g_all.at[l, pl.ds(0, 7)], sem_gs.at[l])
-            wait_all(part.at[l, pl.ds(0, n_chunk // 2)], sem_ds.at[l])
-            wait_all(red.at[l, :, pl.ds(1, 3)], sem_cs.at[l])
+        wait_all(xfin.at[pl.ds(row0, tok), pl.ds(0, model - n_both * cw)], sem_x.at[0])
+        a_copy().wait_send()
+        wait_all(u_all.at[:, pl.ds(0, 7)], sem_us.at[0])
+        wait_all(g_all.at[:, pl.ds(0, 7)], sem_gs.at[0])
+        wait_all(part.at[0, pl.ds(0, n_chunk - n_both // 2)], sem_ds.at[0])
+        wait_all(part.at[0, pl.ds(0, n_both), pl.ds(0, 6)], sem_ds.at[1])
+        wait_all(red.at[:, pl.ds(0, n_chunk - n_both // 2), pl.ds(1, 3)], sem_cs.at[0])
+        wait_all(red.at[:, pl.ds(0, n_both), pl.ds(1, 3)], sem_cs.at[1])
 
 
 def solution(mesh):
@@ -397,6 +451,7 @@
         topk = expert_ids.shape[2]
         cw = 256
         n_chunk = model // cw
+        n_both = n_chunk // 2
         kflat = k_cache.reshape(layers, n_tok, seq * kvh, hd)
         vflat = v_cache.reshape(layers, n_tok, seq * kvh, hd)
         ids = jnp.swapaxes(expert_ids, 1, 2)
@@ -420,9 +475,10 @@
                 vm((layers, n_dev, tok, model), BF16), vm((layers, n_dev, tok, 128), F32), vm((n_loc, n_dev * tok, 128), F32),
                 vm((n_loc, n_dev * tok, ff), BF16), vm((layers, n_chunk, n_dev, tok, cw), F32),
                 vm((layers, n_chunk, 4, tok, cw), F32), vm((layers, n_chunk, 4, tok, cw), F32), vm((layers, n_chunk, 4, tok, cw), F32),
-                vm((tok, model), BF16), pltpu.SMEM((n_tok,), jnp.int32),
-                dma((10,)), dma((2, n_loc // 2)), dma((n_chunk,)), dma((layers, 4)), dma((layers,)), dma((layers,)), dma((layers,)),
-                dma((layers, n_chunk)), dma((layers,)), dma((layers, n_chunk)), dma((layers,)), dma((2,)),
+                vm((n_both, 6, tok, cw), F32), vm((n_both, 4, tok, cw), F32), vm((n_both, 4, 2, tok, cw), F32),
+                vm((2, tok, n_both * cw), BF16), vm((tok, model), BF16), pltpu.SMEM((n_tok,), jnp.int32),
+                dma((10,)), dma((2, n_loc // 2)), dma((n_chunk,)), dma((4,)), dma((1,)), dma((1,)), dma((1,)),
+                dma((n_chunk,)), dma((2,)), dma((n_chunk,)), dma((2,)), dma((4,)),
             ],
             compiler_params=pltpu.CompilerParams(
                 collective_id=0, has_side_effects=True, vmem_limit_bytes=63 * 1024 * 1024),

time: 44.7 us -> 43.6 us (0.975)
  Pallas kernels: 43.9 us -> 42.9 us
    pallas_call x1, Pallas kernels: 43.9 us -> 42.9 us  [body(): pl.pallas_call(functools.partial(kernel, cfg), out_shape=vm((n_tok, model...]
where the time goes in v3:
time: 43.6 us; the launch traced here: 43.5 us
  Pallas kernels  42.9 us (98%)
  local copies, waits for them, and re-layouts  0.63 us (1%)
    pallas_call x1, Pallas kernels, body(): pl.pallas_call(functools.partial(kernel, cfg), out_shape=vm((n_tok, model...  42.9 us

profile of v3, /device:TPU:0, one launch (start us, length us, event | category | flops | bytes accessed | tf_op | source)
XLA Modules:
  0.0 43.5 jit_solution(17232024260224726971)
XLA Ops:
  0.0 42.9 %shard_map.127 = bf16[32,1024]{1,0:T(8,128)(2,1)S(1)} custom-call(bf16[32,1024]{1,0:T(8,128)(2,1)} %hid.1, bf16[2,32,256,128]{3,2,1,0:T(8,128)(2,1)} %bitcast.4, bf16[2,32,256,128]{3,2,1,0:T(8,128)(2,1)} %bitcast.5, s32[32]{0:T(128)} %lens.1, s32[2,8,32]{2,1,0:T(8,128)} %bitcast.7, bf16[2,1024,2048]{2,1,0:T(8,128)(2,1)} %wq.1, bf16[2,1024,256]{2,1,0:T(8,128)(2,1)} %wk.1, ...), custom_call_target="tpu_custom_call" | custom-call | tf_op jit(solution)/shard_map/pallas_call | solution.py:463
  42.9 0.6 %copy.15 = bf16[32,1024]{1,0:T(8,128)(2,1)} copy(bf16[32,1024]{1,0:T(8,128)(2,1)S(1)} %shard_map.127) | data formatting | bytes 131072

commit v4 on v3

--- a/solution.py
+++ b/solution.py
@@ -23,7 +23,7 @@
 def kernel(cfg, hid, kc, vc, lens, ids, wq, wk, wv, wo, wr, wg, wu, wd, xfin,
            wq_s, wk_s, wv_s, wo_s, wr_s, kb, vb, w1_s, w3_s, w2_s,
            x_s, a_s, ids_s, idt_s, q_s, s_s, o_s,
-           u_all, g_all, gb_s, inner_s, part, sbuf, red, rbuf, sbuf2, red2, rbuf2, abuf, hid_s, lens_s,
+           a_all, u_all, g_all, gb_s, inner_s, part, sbuf, red, rbuf, sbuf2, red2, rbuf2, hid_s, lens_s,
            sem_a, sem_w, sem_w2, sem_u, sem_us, sem_g, sem_gs, sem_d, sem_ds, sem_c, sem_cs, sem_x):
     layers, n_pool, n_ep, tok, heads, kvh, hd, seq, n_loc, ff, model = cfg
     n_dev = n_pool * n_ep
@@ -108,6 +108,26 @@
     with jax.named_scope("hidwait"):
         hid_copy.wait()
     x_s[...] = hid_s[...].astype(F32)
+
+    hw = a_all.shape[4]
+
+    def a_copy(l, h, k):
+        view = a_all.at[l, h, me]
+        return pltpu.make_async_remote_copy(
+            src_ref=view, dst_ref=view, send_sem=sem_us.at[0], recv_sem=sem_u.at[2 * k + h if k else 0],
+            device_id=peer(*chips[k], 1)[1], device_id_type=MESH)
+
+    def a_relay(l, h, k):
+        view = a_all.at[l, h, peer(*chips[k], 1)[0]]
+        return pltpu.make_async_remote_copy(
+            src_ref=view, dst_ref=view, send_sem=sem_us.at[0], recv_sem=sem_u.at[0],
+            device_id=peer(0, 0, 1)[1], device_id_type=MESH)
+
+    def a_arrival(l, h, k):
+        view = a_all.at[l, h, peer(*chips[k], 1)[0]]
+        return pltpu.make_async_copy(view, view, sem_u.at[2 * k + h])
+
+    far_first = (3, 1, 2)
 
     scale = hd ** -0.5
     group = heads // kvh
@@ -173,26 +193,19 @@
                 attn_copy(l, 5).wait()
             start_up(0, 1)
             start_up(0, 2)
+        if l == 0:
+            with jax.named_scope("barrier"):
+                pl.semaphore_wait(barrier, len(others))
         oc = 256
         for c in range(model // oc):
             sl = slice(c * oc, (c + 1) * oc)
-            a_s[:, sl] = (x[:, sl] + jnp.dot(o, wo_s[:, sl], preferred_element_type=F32)).astype(BF16).astype(F32)
-
-    def u_copy(l, k):
-        view = u_all.at[l, me]
-        return pltpu.make_async_remote_copy(
-            src_ref=view, dst_ref=view, send_sem=sem_us.at[0], recv_sem=sem_u.at[k],
-            device_id=peer(*chips[k], 1)[1], device_id_type=MESH)
-
-    def u_relay(l, k):
-        view = u_all.at[l, peer(*chips[k], 1)[0]]
-        return pltpu.make_async_remote_copy(
-            src_ref=view, dst_ref=view, send_sem=sem_us.at[0], recv_sem=sem_u.at[0],
-            device_id=peer(0, 0, 1)[1], device_id_type=MESH)
-
-    def u_arrival(l, k):
-        view = u_all.at[l, peer(*chips[k], 1)[0]]
-        return pltpu.make_async_copy(view, view, sem_u.at[k])
+            a = (x[:, sl] + jnp.dot(o, wo_s[:, sl], preferred_element_type=F32)).astype(BF16)
+            a_s[:, sl] = a.astype(F32)
+            h, at = c * oc // hw, c * oc % hw
+            a_all[l, h, me, :, at:at + oc] = a
+            if at + oc == hw:
+                for k in far_first + (0,):
+                    a_copy(l, h, k).start()
 
     def g_copy(l, j):
         view = g_all.at[l, me]
@@ -214,13 +227,8 @@
             src_ref=red.at[l, n, k], dst_ref=rbuf.at[l, n, k], send_sem=sem_cs.at[0], recv_sem=sem_c.at[n],
             device_id=peer(*chips[k], 1)[1], device_id_type=MESH)
 
-    far_first = (3, 1, 2)
-
     def route(l):
         u = rms_normed(a_s[...]).astype(BF16)
-        u_all[l, me] = u
-        for k in far_first + (0,):
-            u_copy(l, k).start()
         if l == 0:
             with jax.named_scope(f"await6_{l}"):
                 attn_copy(l, 6).wait()
@@ -248,7 +256,7 @@
 
     def up_block(l, lo, hi):
         for i in range(lo, hi):
-            ub = u_all[l].reshape(n_tok, model)
+            ub = u_all[...]
             for n in range(ff // fc):
                 sl = slice(n * fc, (n + 1) * fc)
                 one = jnp.dot(ub, w1_s[i, :, sl], preferred_element_type=F32)
@@ -320,11 +328,18 @@
 
     def experts(l):
         with jax.named_scope(f"uwait{l}"):
-            for k in (2, 3, 1):
-                u_arrival(l, k).wait()
-                u_relay(l, k).start()
+            for h in range(2):
+                for k in (2, 3, 1):
+                    a_arrival(l, h, k).wait()
+                    a_relay(l, h, k).start()
         with jax.named_scope(f"urelay{l}"):
-            wait_all(u_all.at[l, pl.ds(0, 4)], sem_u.at[0])
+            wait_all(a_all.at[l, :, pl.ds(0, 4)], sem_u.at[0])
+        for d in range(n_dev):
+            v = [a_all[l, h, d].astype(F32) for h in range(2)]
+            square = sum(jnp.sum(q * q, axis=-1, keepdims=True) for q in v)
+            r = lax.rsqrt(square * (1.0 / model) + EPSILON)
+            for h in range(2):
+                u_all[d * tok:(d + 1) * tok, h * hw:(h + 1) * hw] = (v[h] * r).astype(BF16)
         n_pair = n_loc // 2
         if l > 0:
             down_copy(l, 0).start()
@@ -376,24 +391,17 @@
             src_ref=view, dst_ref=view, send_sem=sem_x.at[0], recv_sem=sem_x.at[1],
             device_id={"pool": other, "ep": ep}, device_id_type=MESH)
 
-    def a_copy():
-        return pltpu.make_async_remote_copy(
-            src_ref=abuf.at[0], dst_ref=abuf.at[1], send_sem=sem_x.at[2], recv_sem=sem_x.at[3],
-            device_id={"pool": other, "ep": ep}, device_id_type=MESH)
-
     def combine(l):
         for n in range(n_chunk):
             sl = slice(n * cw, (n + 1) * cw)
             if both(l, n):
                 m = n - n_chunk + n_both
-                if m == 0:
-                    a_copy().wait_recv()
                 wait_all(rbuf2.at[m, pl.ds(1, 3)], sem_c.at[n])
-                ac = slice(m * cw, (m + 1) * cw)
+                ah, at = n * cw // hw, n * cw % hw
                 for r in range(2):
                     total = part[l, n, peer(*chips[2 * r], 0)[0]] + sbuf2[m, 4 + r]
                     total = (total + rbuf2[m, 2, r]) + (rbuf2[m, 1, r] + rbuf2[m, 3, r])
-                    xfin[pl.ds(orow if r else row0, tok), sl] = (abuf[r, :, ac].astype(F32) + total).astype(BF16)
+                    xfin[pl.ds(orow if r else row0, tok), sl] = (a_all[l, ah, peer(*chips[2 * r], 0)[0], :, at:at + cw].astype(F32) + total).astype(BF16)
                 continue
             total = part[l, n, me] + sbuf[l, n, 0]
             wait_all(rbuf.at[l, n, pl.ds(1, 3)], sem_c.at[n])
@@ -408,16 +416,10 @@
     for l in range(layers):
         with jax.named_scope(f"attention{l}"):
             attention(l)
-        if l == 0:
-            with jax.named_scope("barrier"):
-                pl.semaphore_wait(barrier, len(others))
         with jax.named_scope(f"route{l}"):
             route(l)
         if l == 0:
             start_up(0, 3)
-        if l == layers - 1:
-            abuf[0] = a_s[:, model - n_both * cw:].astype(BF16)
-            a_copy().start()
         experts(l)
         with jax.named_scope(f"combine{l}"):
             combine(l)
@@ -426,8 +428,7 @@
         wait_all(xfin.at[pl.ds(orow, tok), pl.ds(0, model - n_both * cw)], sem_x.at[1])
     with jax.named_scope("drain"):
         wait_all(xfin.at[pl.ds(row0, tok), pl.ds(0, model - n_both * cw)], sem_x.at[0])
-        a_copy().wait_send()
-        wait_all(u_all.at[:, pl.ds(0, 7)], sem_us.at[0])
+        wait_all(a_all.at[:, :, pl.ds(0, 7)], sem_us.at[0])
         wait_all(g_all.at[:, pl.ds(0, 7)], sem_gs.at[0])
         wait_all(part.at[0, pl.ds(0, n_chunk - n_both // 2)], sem_ds.at[0])
         wait_all(part.at[0, pl.ds(0, n_both), pl.ds(0, 6)], sem_ds.at[1])
@@ -472,13 +473,13 @@
                 vm((n_loc, model, ff), BF16), vm((n_loc, model, ff), BF16), vm((n_chunk, n_loc, ff, cw), BF16),
                 vm((tok, model), F32), vm((tok, model), F32), vm((layers, topk, n_tok), jnp.int32), vm((layers, 128, topk), F32),
                 vm((heads * tok, hd), F32), vm((kvh * seq // 128, heads * tok, 128), F32), vm((heads * tok, hd), F32),
-                vm((layers, n_dev, tok, model), BF16), vm((layers, n_dev, tok, 128), F32), vm((n_loc, n_dev * tok, 128), F32),
+                vm((layers, 2, n_dev, tok, model // 2), BF16), vm((n_dev * tok, model), BF16), vm((layers, n_dev, tok, 128), F32), vm((n_loc, n_dev * tok, 128), F32),
                 vm((n_loc, n_dev * tok, ff), BF16), vm((layers, n_chunk, n_dev, tok, cw), F32),
                 vm((layers, n_chunk, 4, tok, cw), F32), vm((layers, n_chunk, 4, tok, cw), F32), vm((layers, n_chunk, 4, tok, cw), F32),
                 vm((n_both, 6, tok, cw), F32), vm((n_both, 4, tok, cw), F32), vm((n_both, 4, 2, tok, cw), F32),
-                vm((2, tok, n_both * cw), BF16), vm((tok, model), BF16), pltpu.SMEM((n_tok,), jnp.int32),
-                dma((10,)), dma((2, n_loc // 2)), dma((n_chunk,)), dma((4,)), dma((1,)), dma((1,)), dma((1,)),
-                dma((n_chunk,)), dma((2,)), dma((n_chunk,)), dma((2,)), dma((4,)),
+                vm((tok, model), BF16), pltpu.SMEM((n_tok,), jnp.int32),
+                dma((10,)), dma((2, n_loc // 2)), dma((n_chunk,)), dma((8,)), dma((1,)), dma((1,)), dma((1,)),
+                dma((n_chunk,)), dma((2,)), dma((n_chunk,)), dma((2,)), dma((2,)),
             ],
             compiler_params=pltpu.CompilerParams(
                 collective_id=0, has_side_effects=True, vmem_limit_bytes=63 * 1024 * 1024),

time: 43.6 us -> 43.2 us (level)
  no operation moved by 1% of the time
where the time goes in v4:
time: 43.2 us; the launch traced here: 43.1 us
  Pallas kernels  42.5 us (98%)
  local copies, waits for them, and re-layouts  0.63 us (1%)
    pallas_call x1, Pallas kernels, body(): pl.pallas_call(functools.partial(kernel, cfg), out_shape=vm((n_tok, model...  42.5 us

profile of v4, /device:TPU:0, one launch (start us, length us, event | category | flops | bytes accessed | tf_op | source)
XLA Modules:
  0.0 43.1 jit_solution(4637583649340693461)
XLA Ops:
  0.0 42.5 %shard_map.127 = bf16[32,1024]{1,0:T(8,128)(2,1)S(1)} custom-call(bf16[32,1024]{1,0:T(8,128)(2,1)} %hid.1, bf16[2,32,256,128]{3,2,1,0:T(8,128)(2,1)} %bitcast.4, bf16[2,32,256,128]{3,2,1,0:T(8,128)(2,1)} %bitcast.5, s32[32]{0:T(128)} %lens.1, s32[2,8,32]{2,1,0:T(8,128)} %bitcast.7, bf16[2,1024,2048]{2,1,0:T(8,128)(2,1)} %wq.1, bf16[2,1024,256]{2,1,0:T(8,128)(2,1)} %wk.1, ...), custom_call_target="tpu_custom_call" | custom-call | tf_op jit(solution)/shard_map/pallas_call | solution.py:464
  42.5 0.6 %copy.15 = bf16[32,1024]{1,0:T(8,128)(2,1)} copy(bf16[32,1024]{1,0:T(8,128)(2,1)S(1)} %shard_map.127) | data formatting | bytes 131072
